TPU v7x, 32 devices: a whole 2x2x4 slice. The times are simulated.
32 devices in a mesh: row: 4 (over y, core), col: 8 (over z, x).
Axes of the slice: x: 2, y: 2, z: 4, core: 2. Of those that a mesh axis runs over, the one named last changes fastest.
Arguments:
- l_saved: bfloat16 [16, 4, 256, 8, 256], P(None, 'row', None, 'col'), as said below
- l_grad: bfloat16 [16, 4, 256, 8, 256], P(None, 'row', None, 'col'), as said below
Outputs:
- grad_out: float32 [16, 4, 256, 8, 256], P(None, 'row', None, 'col')
Inputs may be any that keep to these rules, and one draw needn't show every extreme that they name: Read as one matrix of 16384 rows, l_saved is lower triangular with its diagonal between 1 and 2. Read as one matrix, l_grad is zero above the diagonal.
All inputs are finite; a program needn't handle non-finite values.
Results may differ from a plain program's by a relative error of at most 0.0003.
Values may be sent and summed in bfloat16 or wider, within the bound.
A program may use at most 64 MiB of HBM per device.

v0:
```python
import jax
import jax.numpy as jnp
from jax import lax
from jax.sharding import PartitionSpec as P

HIGH = lax.Precision.HIGHEST


def from_root(array, axis, root):
    mine = lax.axis_index(axis) == root
    return lax.psum(jnp.where(mine, array, jnp.zeros_like(array)), axis)


def right_solve(factor, rhs):
    return lax.linalg.triangular_solve(factor, rhs, left_side=False, lower=True)


def diag_gradient(factor, lower_part):
    eye = jnp.eye(factor.shape[0], dtype=jnp.float32)
    middle = jnp.dot(factor.T, lower_part, precision=HIGH, preferred_element_type=jnp.float32)
    middle = jnp.tril(middle) - 0.5 * middle * eye
    half = lax.linalg.triangular_solve(factor, middle, left_side=True, lower=True, transpose_a=True)
    full = right_solve(factor, half)
    return full + full.T


def stacked_inner(left, right):
    flat_left = left.reshape(-1, left.shape[-1])
    flat_right = right.reshape(-1, right.shape[-1]).astype(jnp.float32)
    return lax.dot_general(
        flat_left,
        flat_right,
        (((0,), (0,)), ((), ())),
        precision=HIGH,
        preferred_element_type=jnp.float32,
    )


def solve_rows(diag_factor, column, below):
    rows_here, tile = (column.shape[0], column.shape[1])
    inverse = right_solve(diag_factor, jnp.eye(tile, dtype=jnp.float32))
    solved = jnp.dot(
        column.reshape(-1, tile), inverse, precision=HIGH, preferred_element_type=jnp.float32
    ).reshape(rows_here, tile, tile)
    return jnp.where(below, solved, jnp.float32(0.0))


def diag_down(piece, owner_row):
    return from_root(piece, "row", owner_row).astype(jnp.float32)


def per_device(l_saved, l_grad):
    rows_here = l_saved.shape[0]
    tile = l_saved.shape[2]
    n_row = lax.axis_size("row")
    n_col = lax.axis_size("col")
    factor = l_saved.reshape(rows_here, tile, tile)
    grad = l_grad.reshape(rows_here, tile, tile).astype(jnp.float32)
    my_row = lax.axis_index("row")
    my_col = lax.axis_index("col")
    tile_rows = jnp.arange(rows_here, dtype=jnp.int32) * n_row + my_row
    eye = jnp.eye(tile, dtype=jnp.float32)
    for panel in (n_col - 1, n_col - 2):
        owner_row = panel % n_row
        local = panel // n_row
        at_owner = my_row == owner_row
        below = (tile_rows > panel)[:, None, None]
        diag_factor = diag_down(factor[local], owner_row)
        cbar = solve_rows(diag_factor, grad, below)
        term = jnp.where(at_owner, grad[local], jnp.float32(0.0)) - stacked_inner(cbar, factor)
        total = lax.psum(term, "row")
        sym = diag_gradient(diag_factor, jnp.tril(total))
        sent = from_root(jnp.concatenate([cbar, sym[None]], 0), "col", panel)
        cbar = sent[:rows_here]
        sym = sent[rows_here]
        row_factor = from_root(factor[local], "row", owner_row).astype(jnp.float32)
        update = jnp.dot(
            cbar.reshape(-1, tile), row_factor, precision=HIGH, preferred_element_type=jnp.float32
        )
        partial_sum = stacked_inner(cbar, factor)
        summed = lax.psum(partial_sum, "row")
        own_row = grad[local] - (
            summed + jnp.dot(sym, row_factor, precision=HIGH, preferred_element_type=jnp.float32)
        )
        updated = grad - update.reshape(rows_here, tile, tile)
        updated = updated.at[local].set(jnp.where(at_owner, own_row, updated[local]))
        abar = jnp.tril(sym) - 0.5 * sym * eye
        panel_col = jnp.where(
            below,
            cbar,
            jnp.where((tile_rows == panel)[:, None, None], abar[None], jnp.float32(0.0)),
        )
        grad = jnp.where(my_col < panel, updated, jnp.where(my_col == panel, panel_col, grad))
    return grad.reshape(l_grad.shape)


def solution(mesh):
    in_specs = (P(None, "row", None, "col", None), P(None, "row", None, "col", None))
    out_specs = P(None, "row", None, "col", None)
    return jax.shard_map(
        per_device, mesh=mesh, in_specs=in_specs, out_specs=out_specs, check_vma=False
    )
```

profile of v0, /device:TPU:0, one launch (start us, length us, event | category | flops | bytes accessed | tf_op | source)
XLA Modules:
  0.0 607.6 jit_solution(4179768059537039904)
XLA Ops:
  6.5 1.6 select_bitcast_fusion.1
  8.3 4.3 convert_element_type.13
  12.6 32.2 %all-reduce.21.cloned.1.call-done = (bf16[256,256]{1,0:T(8,128)(2,1)}, bf16[256,256]{1,0:T(8,128)(2,1)}) async-done(((bf16[256,256]{1,0:T(8,128)(2,1)}, bf16[256,256]{1,0:T(8,128)(2,1)}), (bf16[256,256]{1,0:T(8,128)(2,1)}, bf16[256,256]{1,0:T(8,128)(2,1)})) %all-reduce.21.cloned.1.call-update) | async-done | bytes 262160 | tf_op jit(solution)/shard_map/psum | solution.py:11
  44.8 1.0 fusion.25
  45.9 4.1 while.14
  46.0 0.6 fusion.114
  46.6 1.4 bitcast_dynamic-update-slice_fusion.4
  48.0 0.6 fusion.114
  48.6 1.4 bitcast_dynamic-update-slice_fusion.4
  50.1 19.7 %custom-call.10 = f32[2,128,128]{1,2,0:T(8,128)S(1)} custom-call(f32[2,128,128]{2,1,0:T(8,128)S(1)} %get-tuple-element.71), custom_call_target="InvertDiagBlocksLowerTriangular" | custom-call | tf_op jit(solution)/shard_map/triangular_solve/custom-call.1 | solution.py:15
  70.7 3.8 convolution_bitcast_fusion
  74.6 5.8 copy.9
  80.3 5.0 fusion.5
  85.4 4.7 broadcast_select_fusion
  90.2 27.7 %all-reduce.9.cloned.1.call-done = f32[256,256]{1,0:T(8,128)} async-done(((f32[256,256]{1,0:T(8,128)}), f32[256,256]{1,0:T(8,128)}) %all-reduce.9.cloned.1.call-update) | async-done | bytes 262160 | tf_op jit(solution)/shard_map/psum | solution.py:71
  117.9 1.3 fusion.33
  120.9 0.7 pad_maximum_fusion
  121.7 1.1 copy.4
  122.8 4.7 maximum_select_fusion
  127.5 13.2 %all-reduce.13.cloned.1.call-start = ((), (), s32[]{:S(2)}) async-start(), calls=%async_computation.2 | async-start | bytes 524288 | tf_op jit(solution)/shard_map/psum | solution.py:81
  140.7 4.0 while.15
  141.3 1.4 bitcast_dynamic-update-slice_fusion.5
  143.3 1.4 bitcast_dynamic-update-slice_fusion.5
  144.7 19.7 %custom-call.13 = f32[2,128,128]{1,2,0:T(8,128)S(1)} custom-call(f32[2,128,128]{2,1,0:T(8,128)S(1)} %get-tuple-element.74), custom_call_target="InvertDiagBlocksLowerTriangular" | custom-call | tf_op jit(solution)/shard_map/triangular_solve/custom-call.1 | solution.py:15
  165.3 125.3 %all-reduce.11.cloned.1.call-done = f32[17,256,256]{2,1,0:T(8,128)} async-done(((f32[17,256,256]{2,1,0:T(8,128)}), f32[17,256,256]{2,1,0:T(8,128)}) %all-reduce.11.cloned.1.call-update) | async-done | bytes 4456464 | tf_op jit(solution)/shard_map/psum | solution.py:11
  290.7 2.2 slice-done.3
  292.9 4.1 fusion.83
  297.1 4.9 bitcast_subtract_fusion
  302.0 2.0 copy-done.5
  304.0 1.0 subtract_bitcast_fusion.1
  305.0 23.4 %all-reduce.13.cloned.1.call-done = f32[256,256]{1,0:T(8,128)} async-done(((f32[256,256]{1,0:T(8,128)}), f32[256,256]{1,0:T(8,128)}) %all-reduce.13.cloned.1.call-update) | async-done | bytes 262160 | tf_op jit(solution)/shard_map/psum | solution.py:81
  328.5 2.1 fusion.12
  330.5 5.1 fusion
  335.7 3.7 convolution_select_fusion
  339.4 1.9 copy-done.1
  341.3 4.2 convolution_subtract_fusion.1
  345.6 31.5 %all-reduce.15.cloned.1.call-done = f32[256,256]{1,0:T(8,128)} async-done(((f32[256,256]{1,0:T(8,128)}), f32[256,256]{1,0:T(8,128)}) %all-reduce.15.cloned.1.call-update) | async-done | bytes 262160 | tf_op jit(solution)/shard_map/psum | solution.py:71
  377.1 1.3 fusion.36
  380.3 4.7 maximum_select_fusion.1
  385.3 162.9 %all-reduce.17.cloned.1.call-done = f32[17,256,256]{2,1,0:T(8,128)} async-done(((f32[17,256,256]{2,1,0:T(8,128)}), f32[17,256,256]{2,1,0:T(8,128)}) %all-reduce.17.cloned.1.call-update) | async-done | bytes 4456464 | tf_op jit(solution)/shard_map/psum | solution.py:11
  548.2 2.2 slice-done.2
  550.4 4.1 fusion.84
  554.6 5.6 convolution_subtract_fusion
  560.2 2.0 copy-done.4
  562.3 23.7 %all-reduce.19.cloned.1.call-done = f32[256,256]{1,0:T(8,128)} async-done(((f32[256,256]{1,0:T(8,128)}), f32[256,256]{1,0:T(8,128)}) %all-reduce.19.cloned.1.call-update) | async-done | bytes 262160 | tf_op jit(solution)/shard_map/psum | solution.py:81
  586.0 2.1 fusion.15
  588.1 5.9 select_bitcast_fusion
  594.0 6.3 %copy.7 = f32[16,1,256,1,256]{4,3,2,1,0:T(1,128)} copy(f32[16,1,256,1,256]{4,2,0,3,1:T(8,128)S(1)} %select_bitcast_fusion) | data formatting | bytes 8388608 | tf_op jit(solution)/shard_map/reshape | solution.py:94
  (74 shorter events, 7.7 us)
Async XLA Ops:
  6.5 38.3 %all-reduce.21.cloned.1.call-start = ((), (), s32[]{:S(2)}) async-start(), calls=%async_computation.6 | async-start | bytes 524288 | tf_op jit(solution)/shard_map/psum | solution.py:11
  8.2 109.7 %all-reduce.9.cloned.1.call-start = ((), (), s32[]{:S(2)}) async-start(), calls=%async_computation | async-start | bytes 524288 | tf_op jit(solution)/shard_map/psum | solution.py:71
  8.3 62.4 %copy-start.3 = (bf16[16,1,256,1,256]{4,2,3,1,0:T(8,128)(2,1)S(1)}, bf16[16,1,256,1,256]{4,2,3,1,0:T(8,128)(2,1)}, u32[]{:S(2)}) copy-start(bf16[16,1,256,1,256]{4,2,3,1,0:T(8,128)(2,1)} %param.11) | copy-start | bytes 6291460
  74.6 5.8 copy-start.2
  85.4 205.3 %all-reduce.11.cloned.1.call-start = ((), (), s32[]{:S(2)}) async-start(), calls=%async_computation.1 | async-start | bytes 8912896 | tf_op jit(solution)/shard_map/psum | solution.py:11
  85.4 32.4 %copy-start.7 = (bf16[256,256]{1,0:T(8,128)(2,1)S(1)}, bf16[256,256]{1,0:T(8,128)(2,1)}, u32[]{:S(2)}) copy-start(bf16[256,256]{1,0:T(8,128)(2,1)} %get-tuple-element.93) | copy-start | bytes 393220
  127.5 201.0 %all-reduce.13.cloned.1.call-start = ((), (), s32[]{:S(2)}) async-start(), calls=%async_computation.2 | async-start | bytes 524288 | tf_op jit(solution)/shard_map/psum | solution.py:81
  290.7 2.2 slice-start.3
  297.0 80.1 %all-reduce.15.cloned.1.call-start = ((), (), s32[]{:S(2)}) async-start(), calls=%async_computation.3 | async-start | bytes 524288 | tf_op jit(solution)/shard_map/psum | solution.py:71
  302.0 2.0 copy-start.5
  335.6 3.8 copy-start
  339.4 1.9 copy-start.1
  339.4 37.7 %copy-start.6 = (bf16[256,256]{1,0:T(8,128)(2,1)S(1)}, bf16[256,256]{1,0:T(8,128)(2,1)}, u32[]{:S(2)}) copy-start(bf16[256,256]{1,0:T(8,128)(2,1)} %get-tuple-element.94) | copy-start | bytes 393220
  345.5 202.7 %all-reduce.17.cloned.1.call-start = ((), (), s32[]{:S(2)}) async-start(), calls=%async_computation.4 | async-start | bytes 8912896 | tf_op jit(solution)/shard_map/psum | solution.py:11
  385.1 201.0 %all-reduce.19.cloned.1.call-start = ((), (), s32[]{:S(2)}) async-start(), calls=%async_computation.5 | async-start | bytes 524288 | tf_op jit(solution)/shard_map/psum | solution.py:81
  548.2 2.2 slice-start.2
  550.4 11.8 %slice-start = ((s8[4456448]{0:T(1024)(128)(4,1)}), s8[262144]{0:T(1024)(128)(4,1)S(1)}, s32[]{:S(2)}) async-start(s8[4456448]{0:T(1024)(128)(4,1)} %bitcast.165), calls=%async_computation.7 | async-start | bytes 524288
  554.6 7.7 %slice-start.1 = ((s8[4456448]{0:T(1024)(128)(4,1)}), s8[4194304]{0:T(1024)(128)(4,1)S(1)}, s32[]{:S(2)}) async-start(s8[4456448]{0:T(1024)(128)(4,1)} %bitcast.165), calls=%async_computation.8 | async-start | bytes 8388608
  560.2 2.0 copy-start.4
Sparse Core Ops, SparseCore 0:
  9.7 35.0 all-reduce.20
  85.5 32.3 all-reduce.8
  127.6 163.0 all-reduce.10
  297.1 31.2 all-reduce.12
  345.7 31.3 all-reduce.14
  385.2 163.0 all-reduce.16
  554.7 31.2 all-reduce.18
where the time goes:
time: 616 us; the launch traced here: 608 us
  waiting for transfers between devices  427 us (69%)
  other arithmetic  73.2 us (12%)
  matrix products  47.7 us (8%)
  local copies, waits for them, and re-layouts  31.8 us (5%)
  between operations  14.3 us (2%)
  starting transfers between devices  13.6 us (2%)
    psum x3, waiting for transfers between devices, from_root(): return lax.psum(jnp.where(mine, array, jnp.zeros_like(array)), axis)  320 us
    psum x2, waiting for transfers between devices, per_device(): total = lax.psum(term, 'row')  59.2 us
    psum x2, waiting for transfers between devices, per_device(): summed = lax.psum(partial_sum, 'row')  47.1 us
    another operation x6, other arithmetic, right_solve(): return lax.linalg.triangular_solve(factor, rhs, left_side=False, lower=True)  41.1 us
    dot_general x4, matrix products, stacked_inner(): lax.dot_general(flat_left, flat_right, (((0,), (0,)), ((), ())), precisio...  17.4 us
    psum x2, starting transfers between devices, per_device(): summed = lax.psum(partial_sum, 'row')  13.4 us
  transfers between devices with their start and end apart: 7, of which 7 were waited for; matrix products, arithmetic and copies ran while one was open for 7% of the time, Pallas kernels for 0%

commit v1 on v0

--- a/solution.py
+++ b/solution.py
@@ -68,7 +68,8 @@
         diag_factor = diag_down(factor[local], owner_row)
         cbar = solve_rows(diag_factor, grad, below)
         term = jnp.where(at_owner, grad[local], jnp.float32(0.0)) - stacked_inner(cbar, factor)
-        total = lax.psum(term, "row")
+        shards = lax.all_gather(term, "row")
+        total = jnp.sum(shards, axis=0)
         sym = diag_gradient(diag_factor, jnp.tril(total))
         sent = from_root(jnp.concatenate([cbar, sym[None]], 0), "col", panel)
         cbar = sent[:rows_here]

time: 616 us -> 580 us (0.942)
  waiting for transfers between devices: 427 us -> 390 us
    psum x2 -> x0, waiting for transfers between devices: 59.2 us -> none  [per_device(): total = lax.psum(term, 'row')]
    all_gather x0 -> x2, waiting for transfers between devices: none -> 22.1 us  [per_device(): shards = lax.all_gather(term, 'row')]
  transfers between devices with their start and end apart: 7 -> 7, of which waited for: 7 -> 7; matrix products, arithmetic and copies ran while one was open for 7% -> 9% of each run, Pallas kernels for 0% -> 0%
where the time goes in v1:
time: 580 us; the launch traced here: 572 us
  waiting for transfers between devices  390 us (67%)
  other arithmetic  75.8 us (13%)
  matrix products  44.3 us (8%)
  local copies, waits for them, and re-layouts  33.8 us (6%)
  between operations  14.3 us (2%)
  starting transfers between devices  13.6 us (2%)
    psum x3, waiting for transfers between devices, from_root(): return lax.psum(jnp.where(mine, array, jnp.zeros_like(array)), axis)  320 us
    psum x2, waiting for transfers between devices, per_device(): summed = lax.psum(partial_sum, 'row')  47.1 us
    another operation x6, other arithmetic, right_solve(): return lax.linalg.triangular_solve(factor, rhs, left_side=False, lower=True)  41.1 us
    all_gather x2, waiting for transfers between devices, per_device(): shards = lax.all_gather(term, 'row')  22.1 us
    dot_general x4, matrix products, stacked_inner(): lax.dot_general(flat_left, flat_right, (((0,), (0,)), ((), ())), precisio...  16.3 us
    psum x2, starting transfers between devices, per_device(): summed = lax.psum(partial_sum, 'row')  13.5 us
  transfers between devices with their start and end apart: 7, of which 7 were waited for; matrix products, arithmetic and copies ran while one was open for 9% of the time, Pallas kernels for 0%

profile of v1, /device:TPU:0, one launch (start us, length us, event | category | flops | bytes accessed | tf_op | source)
XLA Modules:
  0.0 571.8 jit_solution(4807855089653112688)
XLA Ops:
  6.5 1.6 select_bitcast_fusion.1
  8.4 4.1 convert_element_type.13
  12.4 32.4 %all-reduce.15.cloned.1.call-done = (bf16[256,256]{1,0:T(8,128)(2,1)}, bf16[256,256]{1,0:T(8,128)(2,1)}) async-done(((bf16[256,256]{1,0:T(8,128)(2,1)}, bf16[256,256]{1,0:T(8,128)(2,1)}), (bf16[256,256]{1,0:T(8,128)(2,1)}, bf16[256,256]{1,0:T(8,128)(2,1)})) %all-reduce.15.cloned.1.call-update) | async-done | bytes 262160 | tf_op jit(solution)/shard_map/psum | solution.py:11
  44.8 1.0 fusion.25
  45.9 4.1 while.14
  46.0 0.7 fusion.114
  46.6 1.4 bitcast_dynamic-update-slice_fusion.4
  48.7 1.4 bitcast_dynamic-update-slice_fusion.4
  50.1 19.7 %custom-call.10 = f32[2,128,128]{1,2,0:T(8,128)S(1)} custom-call(f32[2,128,128]{2,1,0:T(8,128)S(1)} %get-tuple-element.71), custom_call_target="InvertDiagBlocksLowerTriangular" | custom-call | tf_op jit(solution)/shard_map/triangular_solve/custom-call.1 | solution.py:15
  70.7 3.6 convolution_bitcast_fusion
  74.3 1.9 copy-done.2
  76.2 3.9 fusion.5
  80.2 5.7 copy.9
  85.9 4.9 broadcast_select_fusion
  90.8 6.2 %all-gather.5.cloned.1.call-done = f32[1024,256]{1,0:T(8,128)} async-done(((f32[256,256]{1,0:T(8,128)}), f32[1024,256]{1,0:T(8,128)}) %all-gather.5.cloned.1.call-update) | async-done | bytes 1048592 | tf_op jit(solution)/shard_map/all_gather | solution.py:71
  97.0 1.3 reduce_sum.18
  100.4 0.7 pad_maximum_fusion
  101.2 1.1 copy.4
  102.3 4.7 maximum_select_fusion
  107.0 13.2 %all-reduce.9.cloned.1.call-start = ((), (), s32[]{:S(2)}) async-start(), calls=%async_computation.1 | async-start | bytes 524288 | tf_op jit(solution)/shard_map/psum | solution.py:82
  120.3 4.1 while.15
  120.9 1.4 bitcast_dynamic-update-slice_fusion.5
  123.0 1.4 bitcast_dynamic-update-slice_fusion.5
  124.4 19.7 %custom-call.13 = f32[2,128,128]{1,2,0:T(8,128)S(1)} custom-call(f32[2,128,128]{2,1,0:T(8,128)S(1)} %get-tuple-element.74), custom_call_target="InvertDiagBlocksLowerTriangular" | custom-call | tf_op jit(solution)/shard_map/triangular_solve/custom-call.1 | solution.py:15
  145.0 125.1 %all-reduce.7.cloned.1.call-done = f32[17,256,256]{2,1,0:T(8,128)} async-done(((f32[17,256,256]{2,1,0:T(8,128)}), f32[17,256,256]{2,1,0:T(8,128)}) %all-reduce.7.cloned.1.call-update) | async-done | bytes 4456464 | tf_op jit(solution)/shard_map/psum | solution.py:11
  270.2 2.2 slice-done.3
  272.3 4.1 fusion.83
  276.5 4.9 bitcast_subtract_fusion
  281.5 2.0 copy-done.5
  283.5 1.0 subtract_bitcast_fusion.1
  284.5 23.4 %all-reduce.9.cloned.1.call-done = f32[256,256]{1,0:T(8,128)} async-done(((f32[256,256]{1,0:T(8,128)}), f32[256,256]{1,0:T(8,128)}) %all-reduce.9.cloned.1.call-update) | async-done | bytes 262160 | tf_op jit(solution)/shard_map/psum | solution.py:82
  307.9 2.1 fusion.12
  310.0 5.1 fusion
  315.1 3.7 convolution_select_fusion
  318.9 1.9 copy-done.1
  320.8 4.2 convolution_subtract_fusion.1
  325.1 15.9 %all-gather.7.cloned.1.call-done = f32[1024,256]{1,0:T(8,128)} async-done(((f32[256,256]{1,0:T(8,128)}), f32[1024,256]{1,0:T(8,128)}) %all-gather.7.cloned.1.call-update) | async-done | bytes 1048592 | tf_op jit(solution)/shard_map/all_gather | solution.py:71
  340.9 1.3 reduce_sum.19
  344.6 4.7 maximum_select_fusion.1
  349.6 162.9 %all-reduce.11.cloned.1.call-done = f32[17,256,256]{2,1,0:T(8,128)} async-done(((f32[17,256,256]{2,1,0:T(8,128)}), f32[17,256,256]{2,1,0:T(8,128)}) %all-reduce.11.cloned.1.call-update) | async-done | bytes 4456464 | tf_op jit(solution)/shard_map/psum | solution.py:11
  512.5 2.2 slice-done.2
  514.7 4.1 fusion.84
  518.9 5.6 convolution_subtract_fusion
  524.5 2.0 copy-done.4
  526.6 23.7 %all-reduce.13.cloned.1.call-done = f32[256,256]{1,0:T(8,128)} async-done(((f32[256,256]{1,0:T(8,128)}), f32[256,256]{1,0:T(8,128)}) %all-reduce.13.cloned.1.call-update) | async-done | bytes 262160 | tf_op jit(solution)/shard_map/psum | solution.py:82
  550.3 2.1 fusion.15
  552.4 5.9 %select_bitcast_fusion = f32[16,1,256,1,256]{4,2,0,3,1:T(8,128)S(1)} fusion(f32[16,256,256]{2,1,0:T(8,128)} %fusion.15, f32[16,256,256]{2,1,0:T(8,128)} %copy-done, f32[256,256]{1,0:T(8,128)S(1)} %subtract_bitcast_fusion, pred[16]{0:T(512)(128)(4,1)S(1)} %broadcast_compare_fusion, pred[16]{0:T(512)(128)(4,1)S(1)} %get-tuple-element.101, pred[]{:T(512)S(6)} %eq.62, ...), kind=kLoop, calls=%fused_computation.10 | loop fusion | flops 4194304 | bytes 17039394 | tf_op jit(solution)/shard_map/reshape | solution.py:95
  558.3 6.3 %copy.7 = f32[16,1,256,1,256]{4,3,2,1,0:T(1,128)} copy(f32[16,1,256,1,256]{4,2,0,3,1:T(8,128)S(1)} %select_bitcast_fusion) | data formatting | bytes 8388608 | tf_op jit(solution)/shard_map/reshape | solution.py:95
  (76 shorter events, 9.0 us)
Async XLA Ops:
  6.5 38.3 %all-reduce.15.cloned.1.call-start = ((), (), s32[]{:S(2)}) async-start(), calls=%async_computation.6 | async-start | bytes 524288 | tf_op jit(solution)/shard_map/psum | solution.py:11
  8.2 88.8 %all-gather.5.cloned.1.call-start = ((), (), s32[]{:S(2)}) async-start(), calls=%async_computation.4 | async-start | bytes 1310720 | tf_op jit(solution)/shard_map/all_gather | solution.py:71
  45.9 30.3 %copy-start.3 = (bf16[16,1,256,1,256]{4,2,3,1,0:T(8,128)(2,1)S(1)}, bf16[16,1,256,1,256]{4,2,3,1,0:T(8,128)(2,1)}, u32[]{:S(2)}) copy-start(bf16[16,1,256,1,256]{4,2,3,1,0:T(8,128)(2,1)} %param.10) | copy-start | bytes 6291460
  74.3 1.9 copy-start.2
  80.1 190.0 %all-reduce.7.cloned.1.call-start = ((), (), s32[]{:S(2)}) async-start(), calls=%async_computation | async-start | bytes 8912896 | tf_op jit(solution)/shard_map/psum | solution.py:11
  85.9 12.4 %copy-start.7 = (bf16[256,256]{1,0:T(8,128)(2,1)S(1)}, bf16[256,256]{1,0:T(8,128)(2,1)}, u32[]{:S(2)}) copy-start(bf16[256,256]{1,0:T(8,128)(2,1)} %get-tuple-element.93) | copy-start | bytes 393220
  107.0 200.9 %all-reduce.9.cloned.1.call-start = ((), (), s32[]{:S(2)}) async-start(), calls=%async_computation.1 | async-start | bytes 524288 | tf_op jit(solution)/shard_map/psum | solution.py:82
  270.2 2.2 slice-start.3
  276.5 64.5 %all-gather.7.cloned.1.call-start = ((), (), s32[]{:S(2)}) async-start(), calls=%async_computation.5 | async-start | bytes 1310720 | tf_op jit(solution)/shard_map/all_gather | solution.py:71
  281.5 2.0 copy-start.5
  315.1 3.8 copy-start
  318.9 1.9 copy-start.1
  320.8 21.5 %copy-start.6 = (bf16[256,256]{1,0:T(8,128)(2,1)S(1)}, bf16[256,256]{1,0:T(8,128)(2,1)}, u32[]{:S(2)}) copy-start(bf16[256,256]{1,0:T(8,128)(2,1)} %get-tuple-element.94) | copy-start | bytes 393220
  325.0 187.5 %all-reduce.11.cloned.1.call-start = ((), (), s32[]{:S(2)}) async-start(), calls=%async_computation.2 | async-start | bytes 8912896 | tf_op jit(solution)/shard_map/psum | solution.py:11
  349.3 201.0 %all-reduce.13.cloned.1.call-start = ((), (), s32[]{:S(2)}) async-start(), calls=%async_computation.3 | async-start | bytes 524288 | tf_op jit(solution)/shard_map/psum | solution.py:82
  512.5 2.2 slice-start.2
  514.7 11.8 %slice-start = ((s8[4456448]{0:T(1024)(128)(4,1)}), s8[262144]{0:T(1024)(128)(4,1)S(1)}, s32[]{:S(2)}) async-start(s8[4456448]{0:T(1024)(128)(4,1)} %bitcast.167), calls=%async_computation.7 | async-start | bytes 524288
  518.8 7.7 %slice-start.1 = ((s8[4456448]{0:T(1024)(128)(4,1)}), s8[4194304]{0:T(1024)(128)(4,1)S(1)}, s32[]{:S(2)}) async-start(s8[4456448]{0:T(1024)(128)(4,1)} %bitcast.167), calls=%async_computation.8 | async-start | bytes 8388608
  524.5 2.0 copy-start.4
Sparse Core Ops, SparseCore 0:
  9.7 35.0 all-reduce.14
  80.2 16.6 all-gather.4
  107.1 162.9 all-reduce.6
  276.6 31.2 all-reduce.8
  325.1 15.7 all-gather.6
  349.5 163.0 all-reduce.10
  519.0 31.2 all-reduce.12
